TPU v7x, 32 devices: a whole 2x2x4 slice. The times are simulated.
32 devices in a mesh: parts: 2 (over x), rows: 16 (over z, y, core).
Axes of the slice: x: 2, y: 2, z: 4, core: 2. Of those that a mesh axis runs over, the one named last changes fastest.
Arguments:
- pair: bfloat16 [64, 32, 128], P(('parts', 'rows')), parts along dimension 0, may hold values from -16 to 16
- mask: int32 [64], P('parts'), parts along dimension 0, may hold values from 0 to 1, as said below
- w_tri_in: bfloat16 [128, 512], replicated, may hold values from -0.5 to 0.5
- w_tri_gate: bfloat16 [128, 128], replicated, may hold values from -0.5 to 0.5
- w_tri_out: bfloat16 [128, 128], replicated, may hold values from -0.5 to 0.5
- w_qkv: bfloat16 [128, 384], replicated, may hold values from -0.5 to 0.5
- w_att_bias: bfloat16 [128, 4], replicated, may hold values from -80 to 80
- w_att_gate: bfloat16 [128, 128], replicated, may hold values from -0.5 to 0.5
- w_att_out: bfloat16 [128, 128], replicated, may hold values from -0.5 to 0.5
Outputs:
- updated: bfloat16 [64, 32, 128], P(('parts', 'rows')), parts along dimension 0
There are 2 independent parts, one for each index of `parts`. A program takes and returns all parts, laid end to end along the dimension named above; an argument that names none is the same for every part. Nothing has to cross between parts.
Inputs may be any that keep to these rules, and one draw needn't show every extreme that they name: `mask`: 0 on every residue from some L on, with 16 <= L <= 31; before L each residue may be 1 or 0 (unresolved); residue 0 is always 1.
All inputs are finite; a program needn't handle non-finite values.
Results may differ from a plain program's by a relative error of at most 0.012.
Values may be sent and summed in bfloat16 or wider, within the bound.
A program may use at most 64 MiB of HBM per device.

v0:
```python
import jax
import jax.numpy as jnp
from jax import lax
from jax.sharding import PartitionSpec as P

HEADS = 4
HEAD_DIM = 32
EPSILON = 1e-05
MASK_PENALTY = 1000000000.0


def normalize(values, along_axis):
    values = values.astype(jnp.float32)
    center = jnp.mean(values, axis=along_axis, keepdims=True)
    shifted = values - center
    spread = jnp.mean(shifted * shifted, axis=along_axis, keepdims=True)
    return shifted * lax.rsqrt(spread + EPSILON)


def attend(queries, key_rows, values, score_bias, key_penalty, score_scale):
    column_count = queries.shape[1]
    heads_here = queries.shape[2]
    block_size = max(1, 4 // heads_here)

    def reorder(tensor):
        return tensor.reshape(
            tensor.shape[0], column_count // block_size, block_size, heads_here, -1
        ).transpose(1, 0, 2, 3, 4)

    def one_block(inputs):
        query_part, key_part, value_part = inputs
        scores = (
            jnp.einsum("kbhd,ibhd->bhki", key_part, query_part, preferred_element_type=jnp.float32)
            * score_scale
        )
        scores = scores + score_bias[None] + key_penalty[None, None, :, None]
        row_peak = jnp.max(scores, axis=2, keepdims=True)
        weights = jnp.exp(scores - row_peak)
        weights = (weights / jnp.sum(weights, axis=2, keepdims=True)).astype(jnp.bfloat16)
        result = jnp.einsum(
            "bhki,kbhd->ibhd", weights, value_part, preferred_element_type=jnp.float32
        )
        return result.astype(jnp.bfloat16)

    outputs = lax.map(one_block, (reorder(queries), reorder(key_rows), reorder(values)))
    return outputs.transpose(1, 0, 2, 3, 4).reshape(queries.shape)


def local(pair, mask, w_tri_in, w_tri_gate, w_tri_out, w_qkv, w_att_bias, w_att_gate, w_att_out):
    row_count = pair.shape[0]
    residues = pair.shape[1]
    devices = lax.axis_size("rows")
    first_row = lax.axis_index("rows") * row_count
    key_mask = mask.astype(jnp.float32)
    row_mask = lax.dynamic_slice_in_dim(key_mask, first_row, row_count, 0)
    key_penalty = (key_mask - 1.0) * MASK_PENALTY
    normed = normalize(pair, 2).astype(jnp.bfloat16)
    projected = jnp.einsum("rkc,cf->frk", normed, w_tri_in, preferred_element_type=jnp.float32)
    hidden = w_tri_out.shape[0]
    pair_mask = row_mask[:, None] * key_mask[None, :]
    left_side = (
        jax.nn.sigmoid(projected[:hidden]) * projected[hidden : 2 * hidden] * pair_mask
    ).astype(jnp.bfloat16)
    right_side = (
        jax.nn.sigmoid(projected[2 * hidden : 3 * hidden]) * projected[3 * hidden :] * pair_mask
    ).astype(jnp.bfloat16)
    left_cols, right_cols = (
        lax.all_to_all(left_side, "rows", split_axis=0, concat_axis=1, tiled=True),
        lax.all_to_all(right_side, "rows", split_axis=0, concat_axis=1, tiled=True),
    )
    product = jnp.einsum(
        "cik,cjk->cij", left_cols, right_cols, preferred_element_type=jnp.float32
    ).astype(jnp.bfloat16)
    triangle_rows = lax.all_to_all(product, "rows", split_axis=1, concat_axis=0, tiled=True)
    triangle_normed = normalize(triangle_rows, 0).astype(jnp.bfloat16)
    triangle_gate = jax.nn.sigmoid(
        jnp.einsum("rjc,cd->rjd", normed, w_tri_gate, preferred_element_type=jnp.float32)
    )
    triangle_update = jnp.einsum(
        "crj,cd->rjd", triangle_normed, w_tri_out, preferred_element_type=jnp.float32
    )
    middle = lax.optimization_barrier(
        (pair.astype(jnp.float32) + triangle_gate * triangle_update).astype(jnp.bfloat16)
    )
    attention_input = normalize(middle, 2).astype(jnp.bfloat16)
    bias_rows = jnp.einsum(
        "kic,ch->hki", attention_input, w_att_bias, preferred_element_type=jnp.float32
    )
    score_scale = HEAD_DIM ** (-0.5)
    groups = devices // HEADS
    group_width = residues // groups
    projections = jnp.einsum(
        "rgwc,cthd->hgrtwd",
        attention_input.reshape(row_count, groups, group_width, -1),
        w_qkv.reshape(-1, 3, HEADS, HEAD_DIM),
        preferred_element_type=jnp.float32,
    ).astype(jnp.bfloat16)
    outgoing = projections.reshape(devices, row_count, 3, group_width * HEAD_DIM)
    received = lax.all_to_all(outgoing, "rows", split_axis=0, concat_axis=1, tiled=True)
    bias_copies = jnp.repeat(bias_rows, groups, axis=0)
    head_bias = lax.all_to_all(bias_copies, "rows", split_axis=0, concat_axis=1, tiled=True)
    pieces = received.reshape(residues, 3, group_width, 1, HEAD_DIM)
    attended = attend(pieces[:, 0], pieces[:, 1], pieces[:, 2], head_bias, key_penalty, score_scale)
    returned = lax.all_to_all(
        attended.reshape(residues, group_width, HEAD_DIM),
        "rows",
        split_axis=0,
        concat_axis=1,
        tiled=True,
    )
    attention_rows = (
        returned.reshape(row_count, HEADS, groups, group_width, HEAD_DIM)
        .transpose(0, 2, 3, 1, 4)
        .reshape(row_count, residues, HEADS * HEAD_DIM)
    )
    attention_gate = jax.nn.sigmoid(
        jnp.einsum("rjc,cf->rjf", attention_input, w_att_gate, preferred_element_type=jnp.float32)
    )
    gated_output = (attention_gate * attention_rows.astype(jnp.float32)).astype(jnp.bfloat16)
    result = middle.astype(jnp.float32) + jnp.einsum(
        "rjf,fc->rjc", gated_output, w_att_out, preferred_element_type=jnp.float32
    )
    return result.astype(jnp.bfloat16)


def solution(mesh):
    placed = (P(("parts", "rows"), None, None), P("parts"), P(), P(), P(), P(), P(), P(), P())
    return jax.shard_map(
        local,
        mesh=mesh,
        in_specs=placed,
        out_specs=P(("parts", "rows"), None, None),
        check_vma=False,
    )
```

profile of v0, /device:TPU:0, one launch (start us, length us, event | category | flops | bytes accessed | tf_op | source)
XLA Modules:
  0.0 73.1 jit_solution(14103554241699838095)
XLA Ops:
  0.0 0.7 convert_element_type.92
  1.0 0.2 fusion.50
  1.1 0.2 convolution_bitcast_fusion
  1.4 0.1 copy.52
  1.6 0.7 reshape.158
  2.3 7.4 %all-to-all-start = ((bf16[16,2,256]{2,1,0:T(2,128)(2,1)}), bf16[16,2,256]{2,1,0:T(2,128)(2,1)S(1)}, u32[]{:S(2)}, u32[]{:S(2)}) async-start(bf16[16,2,256]{2,1,0:T(2,128)(2,1)} %reshape.158), calls=%async_computation | async-start | bytes 32768 | tf_op jit(solution)/shard_map/all_to_all | solution.py:68
  9.7 0.1 copy.55
  9.8 0.7 reshape.160
  10.5 5.7 %all-to-all-done = bf16[16,2,256]{2,1,0:T(2,128)(2,1)S(1)} async-done(((bf16[16,2,256]{2,1,0:T(2,128)(2,1)}), bf16[16,2,256]{2,1,0:T(2,128)(2,1)S(1)}, u32[]{:S(2)}, u32[]{:S(2)}) %all-to-all-start) | async-done | bytes 16416 | tf_op jit(solution)/shard_map/all_to_all | solution.py:68
  16.2 3.5 %all-to-all-start.1 = ((bf16[16,2,256]{2,1,0:T(2,128)(2,1)}), bf16[16,2,256]{2,1,0:T(2,128)(2,1)S(1)}, u32[]{:S(2)}, u32[]{:S(2)}) async-start(bf16[16,2,256]{2,1,0:T(2,128)(2,1)} %reshape.160), calls=%async_computation.1 | async-start | bytes 32768 | tf_op jit(solution)/shard_map/all_to_all | solution.py:69
  19.7 0.2 fusion.32
  19.9 0.1 reshape.159
  20.1 6.0 %all-to-all-done.1 = bf16[16,2,256]{2,1,0:T(2,128)(2,1)S(1)} async-done(((bf16[16,2,256]{2,1,0:T(2,128)(2,1)}), bf16[16,2,256]{2,1,0:T(2,128)(2,1)S(1)}, u32[]{:S(2)}, u32[]{:S(2)}) %all-to-all-start.1) | async-done | bytes 16416 | tf_op jit(solution)/shard_map/all_to_all | solution.py:69
  26.2 0.1 reshape.161
  26.4 0.2 convolution_convert_fusion.2
  26.6 0.7 reshape.162
  27.3 3.6 %all-to-all-start.2 = ((bf16[16,2,256]{2,1,0:T(2,128)(2,1)}), bf16[16,2,256]{2,1,0:T(2,128)(2,1)S(1)}, u32[]{:S(2)}, u32[]{:S(2)}) async-start(bf16[16,2,256]{2,1,0:T(2,128)(2,1)} %reshape.162), calls=%async_computation.2 | async-start | bytes 32768 | tf_op jit(solution)/shard_map/all_to_all | solution.py:74
  31.0 0.1 copy.61
  31.1 6.3 %all-to-all-done.2 = bf16[16,2,256]{2,1,0:T(2,128)(2,1)S(1)} async-done(((bf16[16,2,256]{2,1,0:T(2,128)(2,1)}), bf16[16,2,256]{2,1,0:T(2,128)(2,1)S(1)}, u32[]{:S(2)}, u32[]{:S(2)}) %all-to-all-start.2) | async-done | bytes 16416 | tf_op jit(solution)/shard_map/all_to_all | solution.py:74
  37.4 0.1 reshape.163
  37.6 0.7 copy-done.4
  38.3 0.2 fusion.33
  38.5 0.1 convert_reduce_fusion
  38.6 0.2 fusion.48
  38.8 0.3 fusion.24
  39.1 0.8 %reshape.157 = bf16[16,2,3,256]{3,1,2,0:T(2,128)(2,1)} reshape(bf16[4,4,2,3,8,32]{5,4,2,3,1,0:T(8,128)(2,1)S(1)} %copy.75) | data formatting | bytes 98304 | tf_op jit(solution)/shard_map/reshape | solution.py:98
  39.9 3.6 %all-to-all-start.3 = ((bf16[16,2,3,256]{3,1,2,0:T(2,128)(2,1)}), bf16[16,2,3,256]{3,1,2,0:T(2,128)(2,1)S(1)}, u32[]{:S(2)}, u32[]{:S(2)}) async-start(bf16[16,2,3,256]{3,1,2,0:T(2,128)(2,1)} %reshape.157), calls=%async_computation.3 | async-start | bytes 98304 | tf_op jit(solution)/shard_map/all_to_all | solution.py:99
  43.6 0.2 convolution_bitcast_fusion.1
  43.8 6.5 %all-to-all-done.3 = bf16[16,2,3,256]{3,1,2,0:T(2,128)(2,1)S(1)} async-done(((bf16[16,2,3,256]{3,1,2,0:T(2,128)(2,1)}), bf16[16,2,3,256]{3,1,2,0:T(2,128)(2,1)S(1)}, u32[]{:S(2)}, u32[]{:S(2)}) %all-to-all-start.3) | async-done | bytes 49184 | tf_op jit(solution)/shard_map/all_to_all | solution.py:99
  50.3 0.6 broadcast_in_dim.8
  50.9 3.5 %all-to-all-start.4 = ((f32[16,2,32]{2,1,0:T(2,128)}), f32[16,2,32]{2,1,0:T(2,128)S(1)}, u32[]{:S(2)}, u32[]{:S(2)}) async-start(f32[16,2,32]{2,1,0:T(2,128)} %bitcast.36), calls=%async_computation.4 | async-start | bytes 32768 | tf_op jit(solution)/shard_map/all_to_all | solution.py:101
  54.4 0.2 reshape.141
  54.6 0.1 copy.65
  54.8 6.1 %all-to-all-done.4 = f32[16,2,32]{2,1,0:T(2,128)S(1)} async-done(((f32[16,2,32]{2,1,0:T(2,128)}), f32[16,2,32]{2,1,0:T(2,128)S(1)}, u32[]{:S(2)}, u32[]{:S(2)}) %all-to-all-start.4) | async-done | bytes 4128 | tf_op jit(solution)/shard_map/all_to_all | solution.py:101
  60.9 1.0 %while.10 = (s32[]{:T(128)}, bf16[2,32,4,1,32]{1,4,2,3,0:T(8,128)(2,1)S(1)}, bf16[2,32,4,1,32]{1,4,2,3,0:T(8,128)(2,1)S(1)}, bf16[2,32,4,1,32]{4,1,2,3,0:T(8,128...) while((s32[]{:T(128)}, ...), condition=%wide.region_9.10_spmd, body=%wide.region_6.9_spmd.sunk | while | flops 835776 | bytes 383573 | solution.py:45
  60.9 0.1 fusion.111
  61.0 0.2 fusion.110
  61.2 0.2 fusion.112
  61.4 0.1 fusion.111
  61.5 0.2 fusion.110
  61.7 0.2 fusion.112
  61.8 0.1 copy.69
  62.0 0.1 reshape.164
  62.1 9.1 %all_to_all.78 = bf16[16,2,256]{2,1,0:T(2,128)(2,1)S(1)} all-to-all(bf16[16,2,256]{2,1,0:T(2,128)(2,1)S(1)} %reshape.164), channel_id=1, replica_groups=mesh['parts'=2,'rows'=16] {'rows'}, dimensions={0} | all-to-all | bytes 32768 | tf_op jit(solution)/shard_map/all_to_all | solution.py:104
  71.1 0.1 reshape.165
  71.4 0.1 reshape.144
  71.5 0.6 copy-done.5
  72.1 0.9 %fusion.35 = bf16[2,32,128]{2,1,0:T(8,128)(2,1)} fusion(f32[2,32,128]{2,1,0:T(8,128)S(1)} %reshape.144, bf16[2,32,128]{2,1,0:T(8,128)(2,1)S(1)} %fusion.33, bf16[128,128]{1,0:T(8,128)(2,1)S(1)} %copy-done.5, bf16[128,128]{1,0:T(8,128)(2,1)S(1)} %copy-done.6, f32[2,32]{1,0:T(2,128)S(1)} %add_rsqrt_fusion, f32[2,32]{1,0:T(2,128)S(1)} %broadcast_multiply_fusion.1), kind=kOutput, calls=%fused_computation.40 | convolution fusion | flops 4292608 | bytes 131584 | tf_op jit(solution)/shard_map/rjf,fc->rjc/dot_general | solution.py:120
  (43 shorter events, 0.9 us)
Async XLA Ops:
  0.0 1.1 %copy-start = (bf16[128,512]{1,0:T(8,128)(2,1)S(1)}, bf16[128,512]{1,0:T(8,128)(2,1)}, u32[]{:S(2)}) copy-start(bf16[128,512]{1,0:T(8,128)(2,1)} %param.13) | copy-start | bytes 393220
  0.0 0.9 %copy-start.1 = (bf16[2,32,128]{2,1,0:T(8,128)(2,1)S(1)}, bf16[2,32,128]{2,1,0:T(8,128)(2,1)}, u32[]{:S(2)}) copy-start(bf16[2,32,128]{2,1,0:T(8,128)(2,1)} %param.11) | copy-start | bytes 49156
  2.3 13.9 %all-to-all-start = ((bf16[16,2,256]{2,1,0:T(2,128)(2,1)}), bf16[16,2,256]{2,1,0:T(2,128)(2,1)S(1)}, u32[]{:S(2)}, u32[]{:S(2)}) async-start(bf16[16,2,256]{2,1,0:T(2,128)(2,1)} %reshape.158), calls=%async_computation | async-start | bytes 32768 | tf_op jit(solution)/shard_map/all_to_all | solution.py:68
  10.5 9.2 %copy-start.3 = (bf16[128,128]{1,0:T(8,128)(2,1)S(1)}, bf16[128,128]{1,0:T(8,128)(2,1)}, u32[]{:S(2)}) copy-start(bf16[128,128]{1,0:T(8,128)(2,1)} %param.14) | copy-start | bytes 98308
  16.2 10.0 %all-to-all-start.1 = ((bf16[16,2,256]{2,1,0:T(2,128)(2,1)}), bf16[16,2,256]{2,1,0:T(2,128)(2,1)S(1)}, u32[]{:S(2)}, u32[]{:S(2)}) async-start(bf16[16,2,256]{2,1,0:T(2,128)(2,1)} %reshape.160), calls=%async_computation.1 | async-start | bytes 32768 | tf_op jit(solution)/shard_map/all_to_all | solution.py:69
  26.5 4.4 %copy-start.2 = (bf16[128,384]{1,0:T(8,128)(2,1)S(1)}, bf16[128,384]{1,0:T(8,128)(2,1)}, u32[]{:S(2)}) copy-start(bf16[128,384]{1,0:T(8,128)(2,1)} %param.16) | copy-start | bytes 294916
  27.3 3.6 %copy-start.8 = (s32[32]{0:T(128)S(1)}, s32[32]{0:T(128)}, u32[]{:S(2)}) copy-start(s32[32]{0:T(128)} %param.12) | copy-start | bytes 388
  27.3 10.1 %all-to-all-start.2 = ((bf16[16,2,256]{2,1,0:T(2,128)(2,1)}), bf16[16,2,256]{2,1,0:T(2,128)(2,1)S(1)}, u32[]{:S(2)}, u32[]{:S(2)}) async-start(bf16[16,2,256]{2,1,0:T(2,128)(2,1)} %reshape.162), calls=%async_computation.2 | async-start | bytes 32768 | tf_op jit(solution)/shard_map/all_to_all | solution.py:74
  37.6 0.8 %copy-start.4 = (bf16[128,128]{1,0:T(8,128)(2,1)S(1)}, bf16[128,128]{1,0:T(8,128)(2,1)}, u32[]{:S(2)}) copy-start(bf16[128,128]{1,0:T(8,128)(2,1)} %param.15) | copy-start | bytes 98308
  39.9 3.6 %copy-start.7 = (bf16[128,4]{0,1:T(4,128)(2,1)S(1)}, bf16[128,4]{0,1:T(4,128)(2,1)}, u32[]{:S(2)}) copy-start(bf16[128,4]{0,1:T(4,128)(2,1)} %param.17) | copy-start | bytes 3076
  39.9 10.4 %all-to-all-start.3 = ((bf16[16,2,3,256]{3,1,2,0:T(2,128)(2,1)}), bf16[16,2,3,256]{3,1,2,0:T(2,128)(2,1)S(1)}, u32[]{:S(2)}, u32[]{:S(2)}) async-start(bf16[16,2,3,256]{3,1,2,0:T(2,128)(2,1)} %reshape.157), calls=%async_computation.3 | async-start | bytes 98304 | tf_op jit(solution)/shard_map/all_to_all | solution.py:99
  50.9 10.0 %all-to-all-start.4 = ((f32[16,2,32]{2,1,0:T(2,128)}), f32[16,2,32]{2,1,0:T(2,128)S(1)}, u32[]{:S(2)}, u32[]{:S(2)}) async-start(f32[16,2,32]{2,1,0:T(2,128)} %bitcast.36), calls=%async_computation.4 | async-start | bytes 32768 | tf_op jit(solution)/shard_map/all_to_all | solution.py:101
  71.4 0.8 %copy-start.5 = (bf16[128,128]{1,0:T(8,128)(2,1)S(1)}, bf16[128,128]{1,0:T(8,128)(2,1)}, u32[]{:S(2)}) copy-start(bf16[128,128]{1,0:T(8,128)(2,1)} %param.19) | copy-start | bytes 98308
  71.4 0.8 %copy-start.6 = (bf16[128,128]{1,0:T(8,128)(2,1)S(1)}, bf16[128,128]{1,0:T(8,128)(2,1)}, u32[]{:S(2)}) copy-start(bf16[128,128]{1,0:T(8,128)(2,1)} %param.18) | copy-start | bytes 98308
where the time goes:
time: 73.7 us; the launch traced here: 73.1 us
  waiting for transfers between devices  30.6 us (42%)
  starting transfers between devices  21.7 us (29%)
  blocking collectives  9.07 us (12%)
  local copies, waits for them, and re-layouts  6.74 us (9%)
  matrix products  3.16 us (4%)
  other arithmetic  1.51 us (2%)
    all_to_all x1, blocking collectives, local(): lax.all_to_all(attended.reshape(residues, group_width, HEAD_DIM), 'rows',...  9.07 us
    all_to_all x1, starting transfers between devices, local(): lax.all_to_all(left_side, 'rows', split_axis=0, concat_axis=1, tiled=True)  7.41 us
    all_to_all x1, waiting for transfers between devices, local(): lax.all_to_all(outgoing, 'rows', split_axis=0, concat_axis=1, tiled=True)  6.51 us
    all_to_all x1, waiting for transfers between devices, local(): lax.all_to_all(product, 'rows', split_axis=1, concat_axis=0, tiled=True)  6.3 us
    all_to_all x1, waiting for transfers between devices, local(): lax.all_to_all(bias_copies, 'rows', split_axis=0, concat_axis=1, tiled=True)  6.08 us
    all_to_all x1, waiting for transfers between devices, local(): lax.all_to_all(right_side, 'rows', split_axis=0, concat_axis=1, tiled=True)  6.03 us
    all_to_all x1, waiting for transfers between devices, local(): lax.all_to_all(left_side, 'rows', split_axis=0, concat_axis=1, tiled=True)  5.67 us
    unnamed x27, local copies, waits for them, and re-layouts  4.13 us
  transfers between devices with their start and end apart: 5, of which 5 were waited for; matrix products, arithmetic and copies ran while one was open for 3% of the time, Pallas kernels for 0%

commit v1 on v0

--- a/solution.py
+++ b/solution.py
@@ -7,6 +7,22 @@
 HEAD_DIM = 32
 EPSILON = 1e-05
 MASK_PENALTY = 1000000000.0
+
+
+def swapped_with_each(x, axis, split, join):
+    ways, here = (lax.axis_size(axis), lax.axis_index(axis))
+    width = x.shape[split] // ways
+    shape = list(x.shape)
+    shape[split] = width
+    height = shape[join]
+    shape[join] = height * ways
+    full = jnp.zeros(shape, x.dtype)
+    for mask in range(ways):
+        part = lax.dynamic_slice_in_dim(x, (here ^ mask) * width, width, axis=split)
+        if mask:
+            part = lax.ppermute(part, axis, [(d, d ^ mask) for d in range(ways)])
+        full = lax.dynamic_update_slice_in_dim(full, part, (here ^ mask) * height, axis=join)
+    return full
 
 
 def normalize(values, along_axis):
@@ -101,13 +117,7 @@
     head_bias = lax.all_to_all(bias_copies, "rows", split_axis=0, concat_axis=1, tiled=True)
     pieces = received.reshape(residues, 3, group_width, 1, HEAD_DIM)
     attended = attend(pieces[:, 0], pieces[:, 1], pieces[:, 2], head_bias, key_penalty, score_scale)
-    returned = lax.all_to_all(
-        attended.reshape(residues, group_width, HEAD_DIM),
-        "rows",
-        split_axis=0,
-        concat_axis=1,
-        tiled=True,
-    )
+    returned = swapped_with_each(attended.reshape(residues, group_width, HEAD_DIM), "rows", 0, 1)
     attention_rows = (
         returned.reshape(row_count, HEADS, groups, group_width, HEAD_DIM)
         .transpose(0, 2, 3, 1, 4)

time: 73.7 us -> 86.9 us (1.18)
  starting transfers between devices: 21.7 us -> 42 us
  blocking collectives: 9.07 us -> 0 us
    ppermute x0 -> x15, starting transfers between devices: none -> 20.4 us  [swapped_with_each(): part = lax.ppermute(part, axis, [(d, d ^ mask) for d in range(ways)])]
    all_to_all x1 -> x0, blocking collectives: 9.07 us -> none  [local(): lax.all_to_all(attended.reshape(residues, group_width, HEAD_DIM), 'rows',...]
    ppermute x0 -> x15, waiting for transfers between devices: none -> 1.85 us  [swapped_with_each(): part = lax.ppermute(part, axis, [(d, d ^ mask) for d in range(ways)])]
    all_to_all x1, waiting for transfers between devices: 6.3 us -> 5.3 us  [local(): lax.all_to_all(product, 'rows', split_axis=1, concat_axis=0, tiled=True)]
    unnamed x27 -> x25, local copies, waits for them, and re-layouts: 4.13 us -> 4.69 us
  transfers between devices with their start and end apart: 5 -> 20, of which waited for: 5 -> 6; matrix products, arithmetic and copies ran while one was open for 3% -> 2% of each run, Pallas kernels for 0% -> 0%
where the time goes in v1:
time: 86.9 us; the launch traced here: 86.3 us
  starting transfers between devices  42 us (48%)
  waiting for transfers between devices  31.4 us (36%)
  local copies, waits for them, and re-layouts  7.53 us (9%)
  matrix products  3.15 us (4%)
  other arithmetic  1.51 us (2%)
    ppermute x15, starting transfers between devices, swapped_with_each(): part = lax.ppermute(part, axis, [(d, d ^ mask) for d in range(ways)])  20.4 us
    all_to_all x1, starting transfers between devices, local(): lax.all_to_all(left_side, 'rows', split_axis=0, concat_axis=1, tiled=True)  7.41 us
    all_to_all x1, waiting for transfers between devices, local(): lax.all_to_all(outgoing, 'rows', split_axis=0, concat_axis=1, tiled=True)  6.51 us
    all_to_all x1, waiting for transfers between devices, local(): lax.all_to_all(bias_copies, 'rows', split_axis=0, concat_axis=1, tiled=True)  6.08 us
    all_to_all x1, waiting for transfers between devices, local(): lax.all_to_all(right_side, 'rows', split_axis=0, concat_axis=1, tiled=True)  6.03 us
    all_to_all x1, waiting for transfers between devices, local(): lax.all_to_all(left_side, 'rows', split_axis=0, concat_axis=1, tiled=True)  5.67 us
    all_to_all x1, waiting for transfers between devices, local(): lax.all_to_all(product, 'rows', split_axis=1, concat_axis=0, tiled=True)  5.3 us
    unnamed x25, local copies, waits for them, and re-layouts  4.69 us
  transfers between devices with their start and end apart: 20, of which 6 were waited for; matrix products, arithmetic and copies ran while one was open for 2% of the time, Pallas kernels for 0%

profile of v1, /device:TPU:0, one launch (start us, length us, event | category | flops | bytes accessed | tf_op | source)
XLA Modules:
  0.0 86.3 jit_solution(13476869169215087440)
XLA Ops:
  0.0 0.7 convert_element_type.89
  1.0 0.2 fusion.50
  1.1 0.2 convolution_bitcast_fusion
  1.6 0.7 reshape.156
  2.3 7.4 %all-to-all-start = ((bf16[16,2,256]{2,1,0:T(2,128)(2,1)}), bf16[16,2,256]{2,1,0:T(2,128)(2,1)S(1)}, u32[]{:S(2)}, u32[]{:S(2)}) async-start(bf16[16,2,256]{2,1,0:T(2,128)(2,1)} %reshape.156), calls=%async_computation | async-start | bytes 32768 | tf_op jit(solution)/shard_map/all_to_all | solution.py:84
  9.8 0.7 reshape.158
  10.5 5.7 %all-to-all-done = bf16[16,2,256]{2,1,0:T(2,128)(2,1)S(1)} async-done(((bf16[16,2,256]{2,1,0:T(2,128)(2,1)}), bf16[16,2,256]{2,1,0:T(2,128)(2,1)S(1)}, u32[]{:S(2)}, u32[]{:S(2)}) %all-to-all-start) | async-done | bytes 16416 | tf_op jit(solution)/shard_map/all_to_all | solution.py:84
  16.2 3.4 %all-to-all-start.1 = ((bf16[16,2,256]{2,1,0:T(2,128)(2,1)}), bf16[16,2,256]{2,1,0:T(2,128)(2,1)S(1)}, u32[]{:S(2)}, u32[]{:S(2)}) async-start(bf16[16,2,256]{2,1,0:T(2,128)(2,1)} %reshape.158), calls=%async_computation.1 | async-start | bytes 32768 | tf_op jit(solution)/shard_map/all_to_all | solution.py:85
  19.7 0.2 fusion.32
  20.1 6.0 %all-to-all-done.1 = bf16[16,2,256]{2,1,0:T(2,128)(2,1)S(1)} async-done(((bf16[16,2,256]{2,1,0:T(2,128)(2,1)}), bf16[16,2,256]{2,1,0:T(2,128)(2,1)S(1)}, u32[]{:S(2)}, u32[]{:S(2)}) %all-to-all-start.1) | async-done | bytes 16416 | tf_op jit(solution)/shard_map/all_to_all | solution.py:85
  26.5 0.7 reshape.160
  27.2 3.6 %all-to-all-start.2 = ((bf16[16,2,256]{2,1,0:T(2,128)(2,1)}), bf16[16,2,256]{2,1,0:T(2,128)(2,1)S(1)}, u32[]{:S(2)}, u32[]{:S(2)}) async-start(bf16[16,2,256]{2,1,0:T(2,128)(2,1)} %reshape.160), calls=%async_computation.2 | async-start | bytes 32768 | tf_op jit(solution)/shard_map/all_to_all | solution.py:90
  31.0 0.8 copy-done.2
  32.0 5.3 %all-to-all-done.2 = bf16[16,2,256]{2,1,0:T(2,128)(2,1)S(1)} async-done(((bf16[16,2,256]{2,1,0:T(2,128)(2,1)}), bf16[16,2,256]{2,1,0:T(2,128)(2,1)S(1)}, u32[]{:S(2)}, u32[]{:S(2)}) %all-to-all-start.2) | async-done | bytes 16416 | tf_op jit(solution)/shard_map/all_to_all | solution.py:90
  37.5 0.7 copy-done.4
  38.2 0.2 fusion.33
  38.5 0.2 fusion.48
  38.7 0.3 fusion.24
  39.1 0.8 reshape.155
  39.8 3.6 %all-to-all-start.3 = ((bf16[16,2,3,256]{3,1,2,0:T(2,128)(2,1)}), bf16[16,2,3,256]{3,1,2,0:T(2,128)(2,1)S(1)}, u32[]{:S(2)}, u32[]{:S(2)}) async-start(bf16[16,2,3,256]{3,1,2,0:T(2,128)(2,1)} %reshape.155), calls=%async_computation.3 | async-start | bytes 98304 | tf_op jit(solution)/shard_map/all_to_all | solution.py:115
  43.5 0.2 convolution_bitcast_fusion.1
  43.7 6.5 %all-to-all-done.3 = bf16[16,2,3,256]{3,1,2,0:T(2,128)(2,1)S(1)} async-done(((bf16[16,2,3,256]{3,1,2,0:T(2,128)(2,1)}), bf16[16,2,3,256]{3,1,2,0:T(2,128)(2,1)S(1)}, u32[]{:S(2)}, u32[]{:S(2)}) %all-to-all-start.3) | async-done | bytes 49184 | tf_op jit(solution)/shard_map/all_to_all | solution.py:115
  50.2 0.6 broadcast_in_dim.11
  50.8 3.5 %all-to-all-start.4 = ((f32[16,2,32]{2,1,0:T(2,128)}), f32[16,2,32]{2,1,0:T(2,128)S(1)}, u32[]{:S(2)}, u32[]{:S(2)}) async-start(f32[16,2,32]{2,1,0:T(2,128)} %bitcast.36), calls=%async_computation.4 | async-start | bytes 32768 | tf_op jit(solution)/shard_map/all_to_all | solution.py:117
  54.3 0.2 reshape.140
  54.7 6.1 %all-to-all-done.4 = f32[16,2,32]{2,1,0:T(2,128)S(1)} async-done(((f32[16,2,32]{2,1,0:T(2,128)}), f32[16,2,32]{2,1,0:T(2,128)S(1)}, u32[]{:S(2)}, u32[]{:S(2)}) %all-to-all-start.4) | async-done | bytes 4128 | tf_op jit(solution)/shard_map/all_to_all | solution.py:117
  60.8 1.0 %while.10 = (s32[]{:T(128)}, bf16[2,32,4,1,32]{1,4,2,3,0:T(8,128)(2,1)S(1)}, bf16[2,32,4,1,32]{1,4,2,3,0:T(8,128)(2,1)S(1)}, bf16[2,32,4,1,32]{4,1,2,3,0:T(8,128...) while((s32[]{:T(128)}, ...), condition=%wide.region_9.10_spmd, body=%wide.region_6.9_spmd.sunk | while | flops 835776 | bytes 383573 | solution.py:61
  60.9 0.2 fusion.110
  61.1 0.2 fusion.112
  61.4 0.2 fusion.110
  61.6 0.2 fusion.112
  62.1 0.5 collective-permute-start.1
  62.7 1.3 %collective-permute-start.2 = (bf16[2,8,32]{2,1,0:T(8,128)(2,1)S(1)}, bf16[2,8,32]{2,1,0:T(8,128)(2,1)S(1)}, u32[]{:S(2)}, u32[]{:S(2)}) collective-permute-start(bf16[2,8,32]{2,1,0:T(8,128)(2,1)S(1)} %get-tuple-element.74), channel_id=1, source_target_pairs={{0,3},{1,2},{2,1},{3,0},{4,7},{5,6},{6,5},{7,4},{8,11},{9,10},{10,... | collective-permute-start | bytes 3080 | tf_op jit(solution)/shard_map/ppermute | solution.py:23
  63.9 0.5 collective-permute-start.3
  64.4 1.3 %collective-permute-start.4 = (bf16[2,8,32]{2,1,0:T(8,128)(2,1)S(1)}, bf16[2,8,32]{2,1,0:T(8,128)(2,1)S(1)}, u32[]{:S(2)}, u32[]{:S(2)}) collective-permute-start(bf16[2,8,32]{2,1,0:T(8,128)(2,1)S(1)} %get-tuple-element.72), channel_id=1, source_target_pairs={{0,5},{1,4},{2,7},{3,6},{4,1},{5,0},{6,3},{7,2},{8,13},{9,12},{10,... | collective-permute-start | bytes 3080 | tf_op jit(solution)/shard_map/ppermute | solution.py:23
  65.7 0.5 collective-permute-start.5
  66.2 2.1 %collective-permute-start.6 = (bf16[2,8,32]{2,1,0:T(8,128)(2,1)S(1)}, bf16[2,8,32]{2,1,0:T(8,128)(2,1)S(1)}, u32[]{:S(2)}, u32[]{:S(2)}) collective-permute-start(bf16[2,8,32]{2,1,0:T(8,128)(2,1)S(1)} %get-tuple-element.70), channel_id=1, source_target_pairs={{0,7},{1,6},{2,5},{3,4},{4,3},{5,2},{6,1},{7,0},{8,15},{9,14},{10,... | collective-permute-start | bytes 3080 | tf_op jit(solution)/shard_map/ppermute | solution.py:23
  68.3 0.5 collective-permute-start.7
  68.8 2.2 %collective-permute-start.8 = (bf16[2,8,32]{2,1,0:T(8,128)(2,1)S(1)}, bf16[2,8,32]{2,1,0:T(8,128)(2,1)S(1)}, u32[]{:S(2)}, u32[]{:S(2)}) collective-permute-start(bf16[2,8,32]{2,1,0:T(8,128)(2,1)S(1)} %get-tuple-element.68), channel_id=1, source_target_pairs={{0,9},{1,8},{2,11},{3,10},{4,13},{5,12},{6,15},{7,14},{8,1},{9,0},... | collective-permute-start | bytes 3080 | tf_op jit(solution)/shard_map/ppermute | solution.py:23
  71.0 0.5 collective-permute-start.9
  71.5 3.0 %collective-permute-start.10 = (bf16[2,8,32]{2,1,0:T(8,128)(2,1)S(1)}, bf16[2,8,32]{2,1,0:T(8,128)(2,1)S(1)}, u32[]{:S(2)}, u32[]{:S(2)}) collective-permute-start(bf16[2,8,32]{2,1,0:T(8,128)(2,1)S(1)} %get-tuple-element.66), channel_id=1, source_target_pairs={{0,11},{1,10},{2,9},{3,8},{4,15},{5,14},{6,13},{7,12},{8,3},{9,2},... | collective-permute-start | bytes 3080 | tf_op jit(solution)/shard_map/ppermute | solution.py:23
  74.6 0.5 collective-permute-start.11
  75.1 3.1 %collective-permute-start.12 = (bf16[2,8,32]{2,1,0:T(8,128)(2,1)S(1)}, bf16[2,8,32]{2,1,0:T(8,128)(2,1)S(1)}, u32[]{:S(2)}, u32[]{:S(2)}) collective-permute-start(bf16[2,8,32]{2,1,0:T(8,128)(2,1)S(1)} %get-tuple-element.64), channel_id=1, source_target_pairs={{0,13},{1,12},{2,15},{3,14},{4,9},{5,8},{6,11},{7,10},{8,5},{9,4},... | collective-permute-start | bytes 3080 | tf_op jit(solution)/shard_map/ppermute | solution.py:23
  78.2 0.5 collective-permute-start.13
  78.7 3.9 %collective-permute-start.14 = (bf16[2,8,32]{2,1,0:T(8,128)(2,1)S(1)}, bf16[2,8,32]{2,1,0:T(8,128)(2,1)S(1)}, u32[]{:S(2)}, u32[]{:S(2)}) collective-permute-start(bf16[2,8,32]{2,1,0:T(8,128)(2,1)S(1)} %get-tuple-element.62), channel_id=1, source_target_pairs={{0,15},{1,14},{2,13},{3,12},{4,11},{5,10},{6,9},{7,8},{8,7},{9,6},... | collective-permute-start | bytes 3080 | tf_op jit(solution)/shard_map/ppermute | solution.py:23
  82.7 1.8 %collective-permute-done.13 = bf16[2,8,32]{2,1,0:T(8,128)(2,1)S(1)} collective-permute-done((bf16[2,8,32]{2,1,0:T(8,128)(2,1)S(1)}, bf16[2,8,32]{2,1,0:T(8,128)(2,1)S(1)}, u32[]{:S(2)}, u32[]{:S(2)}) %collective-permute-start.13) | collective-permute-done | bytes 1056 | tf_op jit(solution)/shard_map/ppermute | solution.py:23
  84.8 0.6 copy-done.5
  85.4 0.9 %fusion.35 = bf16[2,32,128]{2,1,0:T(8,128)(2,1)} fusion(f32[2,32,128]{2,1,0:T(8,128)S(1)} %reshape.143, bf16[2,32,128]{2,1,0:T(8,128)(2,1)S(1)} %fusion.33, bf16[128,128]{1,0:T(8,128)(2,1)S(1)} %copy-done.5, bf16[128,128]{1,0:T(8,128)(2,1)S(1)} %copy-done.6, f32[2,32]{1,0:T(2,128)S(1)} %add_rsqrt_fusion, f32[2,32]{1,0:T(2,128)S(1)} %broadcast_multiply_fusion.1), kind=kOutput, calls=%fused_computation.40 | convolution fusion | flops 4292608 | bytes 131584 | tf_op jit(solution)/shard_map/rjf,fc->rjc/dot_general | solution.py:130
  (87 shorter events, 2.8 us)
Async XLA Ops:
  0.0 1.1 %copy-start = (bf16[128,512]{1,0:T(8,128)(2,1)S(1)}, bf16[128,512]{1,0:T(8,128)(2,1)}, u32[]{:S(2)}) copy-start(bf16[128,512]{1,0:T(8,128)(2,1)} %param.13) | copy-start | bytes 393220
  0.0 0.9 copy-start.1
  2.3 13.9 %all-to-all-start = ((bf16[16,2,256]{2,1,0:T(2,128)(2,1)}), bf16[16,2,256]{2,1,0:T(2,128)(2,1)S(1)}, u32[]{:S(2)}, u32[]{:S(2)}) async-start(bf16[16,2,256]{2,1,0:T(2,128)(2,1)} %reshape.156), calls=%async_computation | async-start | bytes 32768 | tf_op jit(solution)/shard_map/all_to_all | solution.py:84
  10.5 9.1 %copy-start.3 = (bf16[128,128]{1,0:T(8,128)(2,1)S(1)}, bf16[128,128]{1,0:T(8,128)(2,1)}, u32[]{:S(2)}) copy-start(bf16[128,128]{1,0:T(8,128)(2,1)} %param.14) | copy-start | bytes 98308
  16.2 9.9 %all-to-all-start.1 = ((bf16[16,2,256]{2,1,0:T(2,128)(2,1)}), bf16[16,2,256]{2,1,0:T(2,128)(2,1)S(1)}, u32[]{:S(2)}, u32[]{:S(2)}) async-start(bf16[16,2,256]{2,1,0:T(2,128)(2,1)} %reshape.158), calls=%async_computation.1 | async-start | bytes 32768 | tf_op jit(solution)/shard_map/all_to_all | solution.py:85
  27.2 3.6 %copy-start.8 = (s32[32]{0:T(128)S(1)}, s32[32]{0:T(128)}, u32[]{:S(2)}) copy-start(s32[32]{0:T(128)} %param.12) | copy-start | bytes 388
  27.2 10.1 %all-to-all-start.2 = ((bf16[16,2,256]{2,1,0:T(2,128)(2,1)}), bf16[16,2,256]{2,1,0:T(2,128)(2,1)S(1)}, u32[]{:S(2)}, u32[]{:S(2)}) async-start(bf16[16,2,256]{2,1,0:T(2,128)(2,1)} %reshape.160), calls=%async_computation.2 | async-start | bytes 32768 | tf_op jit(solution)/shard_map/all_to_all | solution.py:90
  30.9 0.9 %copy-start.2 = (bf16[128,384]{1,0:T(8,128)(2,1)S(1)}, bf16[128,384]{1,0:T(8,128)(2,1)}, u32[]{:S(2)}) copy-start(bf16[128,384]{1,0:T(8,128)(2,1)} %param.16) | copy-start | bytes 294916
  37.5 0.8 copy-start.4
  39.8 3.6 %copy-start.7 = (bf16[128,4]{0,1:T(4,128)(2,1)S(1)}, bf16[128,4]{0,1:T(4,128)(2,1)}, u32[]{:S(2)}) copy-start(bf16[128,4]{0,1:T(4,128)(2,1)} %param.17) | copy-start | bytes 3076
  39.8 10.4 %all-to-all-start.3 = ((bf16[16,2,3,256]{3,1,2,0:T(2,128)(2,1)}), bf16[16,2,3,256]{3,1,2,0:T(2,128)(2,1)S(1)}, u32[]{:S(2)}, u32[]{:S(2)}) async-start(bf16[16,2,3,256]{3,1,2,0:T(2,128)(2,1)} %reshape.155), calls=%async_computation.3 | async-start | bytes 98304 | tf_op jit(solution)/shard_map/all_to_all | solution.py:115
  50.8 10.0 %all-to-all-start.4 = ((f32[16,2,32]{2,1,0:T(2,128)}), f32[16,2,32]{2,1,0:T(2,128)S(1)}, u32[]{:S(2)}, u32[]{:S(2)}) async-start(f32[16,2,32]{2,1,0:T(2,128)} %bitcast.36), calls=%async_computation.4 | async-start | bytes 32768 | tf_op jit(solution)/shard_map/all_to_all | solution.py:117
  62.0 3.7 %collective-permute-start = (bf16[2,8,32]{2,1,0:T(8,128)(2,1)S(1)}, bf16[2,8,32]{2,1,0:T(8,128)(2,1)S(1)}, u32[]{:S(2)}, u32[]{:S(2)}) collective-permute-start(bf16[2,8,32]{2,1,0:T(8,128)(2,1)S(1)} %get-tuple-element.76), channel_id=1, source_target_pairs={{0,1},{1,0},{2,3},{3,2},{4,5},{5,4},{6,7},{7,6},{8,9},{9,8},{10,11... | collective-permute-start | bytes 3080 | tf_op jit(solution)/shard_map/ppermute | solution.py:23
  62.1 4.0 %collective-permute-start.1 = (bf16[2,8,32]{2,1,0:T(8,128)(2,1)S(1)}, bf16[2,8,32]{2,1,0:T(8,128)(2,1)S(1)}, u32[]{:S(2)}, u32[]{:S(2)}) collective-permute-start(bf16[2,8,32]{2,1,0:T(8,128)(2,1)S(1)} %get-tuple-element.75), channel_id=1, source_target_pairs={{0,2},{1,3},{2,0},{3,1},{4,6},{5,7},{6,4},{7,5},{8,10},{9,11},{10,... | collective-permute-start | bytes 3080 | tf_op jit(solution)/shard_map/ppermute | solution.py:23
  62.7 5.7 %collective-permute-start.2 = (bf16[2,8,32]{2,1,0:T(8,128)(2,1)S(1)}, bf16[2,8,32]{2,1,0:T(8,128)(2,1)S(1)}, u32[]{:S(2)}, u32[]{:S(2)}) collective-permute-start(bf16[2,8,32]{2,1,0:T(8,128)(2,1)S(1)} %get-tuple-element.74), channel_id=1, source_target_pairs={{0,3},{1,2},{2,1},{3,0},{4,7},{5,6},{6,5},{7,4},{8,11},{9,10},{10,... | collective-permute-start | bytes 3080 | tf_op jit(solution)/shard_map/ppermute | solution.py:23
  63.9 4.9 %collective-permute-start.3 = (bf16[2,8,32]{2,1,0:T(8,128)(2,1)S(1)}, bf16[2,8,32]{2,1,0:T(8,128)(2,1)S(1)}, u32[]{:S(2)}, u32[]{:S(2)}) collective-permute-start(bf16[2,8,32]{2,1,0:T(8,128)(2,1)S(1)} %get-tuple-element.73), channel_id=1, source_target_pairs={{0,4},{1,5},{2,6},{3,7},{4,0},{5,1},{6,2},{7,3},{8,12},{9,13},{10,... | collective-permute-start | bytes 3080 | tf_op jit(solution)/shard_map/ppermute | solution.py:23
  64.4 6.7 %collective-permute-start.4 = (bf16[2,8,32]{2,1,0:T(8,128)(2,1)S(1)}, bf16[2,8,32]{2,1,0:T(8,128)(2,1)S(1)}, u32[]{:S(2)}, u32[]{:S(2)}) collective-permute-start(bf16[2,8,32]{2,1,0:T(8,128)(2,1)S(1)} %get-tuple-element.72), channel_id=1, source_target_pairs={{0,5},{1,4},{2,7},{3,6},{4,1},{5,0},{6,3},{7,2},{8,13},{9,12},{10,... | collective-permute-start | bytes 3080 | tf_op jit(solution)/shard_map/ppermute | solution.py:23
  65.7 5.8 %collective-permute-start.5 = (bf16[2,8,32]{2,1,0:T(8,128)(2,1)S(1)}, bf16[2,8,32]{2,1,0:T(8,128)(2,1)S(1)}, u32[]{:S(2)}, u32[]{:S(2)}) collective-permute-start(bf16[2,8,32]{2,1,0:T(8,128)(2,1)S(1)} %get-tuple-element.71), channel_id=1, source_target_pairs={{0,6},{1,7},{2,4},{3,5},{4,2},{5,3},{6,0},{7,1},{8,14},{9,15},{10,... | collective-permute-start | bytes 3080 | tf_op jit(solution)/shard_map/ppermute | solution.py:23
  66.2 8.4 %collective-permute-start.6 = (bf16[2,8,32]{2,1,0:T(8,128)(2,1)S(1)}, bf16[2,8,32]{2,1,0:T(8,128)(2,1)S(1)}, u32[]{:S(2)}, u32[]{:S(2)}) collective-permute-start(bf16[2,8,32]{2,1,0:T(8,128)(2,1)S(1)} %get-tuple-element.70), channel_id=1, source_target_pairs={{0,7},{1,6},{2,5},{3,4},{4,3},{5,2},{6,1},{7,0},{8,15},{9,14},{10,... | collective-permute-start | bytes 3080 | tf_op jit(solution)/shard_map/ppermute | solution.py:23
  68.3 6.7 %collective-permute-start.7 = (bf16[2,8,32]{2,1,0:T(8,128)(2,1)S(1)}, bf16[2,8,32]{2,1,0:T(8,128)(2,1)S(1)}, u32[]{:S(2)}, u32[]{:S(2)}) collective-permute-start(bf16[2,8,32]{2,1,0:T(8,128)(2,1)S(1)} %get-tuple-element.69), channel_id=1, source_target_pairs={{0,8},{1,9},{2,10},{3,11},{4,12},{5,13},{6,14},{7,15},{8,0},{9,1},... | collective-permute-start | bytes 3080 | tf_op jit(solution)/shard_map/ppermute | solution.py:23
  68.8 9.3 %collective-permute-start.8 = (bf16[2,8,32]{2,1,0:T(8,128)(2,1)S(1)}, bf16[2,8,32]{2,1,0:T(8,128)(2,1)S(1)}, u32[]{:S(2)}, u32[]{:S(2)}) collective-permute-start(bf16[2,8,32]{2,1,0:T(8,128)(2,1)S(1)} %get-tuple-element.68), channel_id=1, source_target_pairs={{0,9},{1,8},{2,11},{3,10},{4,13},{5,12},{6,15},{7,14},{8,1},{9,0},... | collective-permute-start | bytes 3080 | tf_op jit(solution)/shard_map/ppermute | solution.py:23
  71.0 7.6 %collective-permute-start.9 = (bf16[2,8,32]{2,1,0:T(8,128)(2,1)S(1)}, bf16[2,8,32]{2,1,0:T(8,128)(2,1)S(1)}, u32[]{:S(2)}, u32[]{:S(2)}) collective-permute-start(bf16[2,8,32]{2,1,0:T(8,128)(2,1)S(1)} %get-tuple-element.67), channel_id=1, source_target_pairs={{0,10},{1,11},{2,8},{3,9},{4,14},{5,15},{6,12},{7,13},{8,2},{9,3},... | collective-permute-start | bytes 3080 | tf_op jit(solution)/shard_map/ppermute | solution.py:23
  71.5 11.1 %collective-permute-start.10 = (bf16[2,8,32]{2,1,0:T(8,128)(2,1)S(1)}, bf16[2,8,32]{2,1,0:T(8,128)(2,1)S(1)}, u32[]{:S(2)}, u32[]{:S(2)}) collective-permute-start(bf16[2,8,32]{2,1,0:T(8,128)(2,1)S(1)} %get-tuple-element.66), channel_id=1, source_target_pairs={{0,11},{1,10},{2,9},{3,8},{4,15},{5,14},{6,13},{7,12},{8,3},{9,2},... | collective-permute-start | bytes 3080 | tf_op jit(solution)/shard_map/ppermute | solution.py:23
  74.6 8.0 %collective-permute-start.11 = (bf16[2,8,32]{2,1,0:T(8,128)(2,1)S(1)}, bf16[2,8,32]{2,1,0:T(8,128)(2,1)S(1)}, u32[]{:S(2)}, u32[]{:S(2)}) collective-permute-start(bf16[2,8,32]{2,1,0:T(8,128)(2,1)S(1)} %get-tuple-element.65), channel_id=1, source_target_pairs={{0,12},{1,13},{2,14},{3,15},{4,8},{5,9},{6,10},{7,11},{8,4},{9,5},... | collective-permute-start | bytes 3080 | tf_op jit(solution)/shard_map/ppermute | solution.py:23
  75.1 7.6 %collective-permute-start.12 = (bf16[2,8,32]{2,1,0:T(8,128)(2,1)S(1)}, bf16[2,8,32]{2,1,0:T(8,128)(2,1)S(1)}, u32[]{:S(2)}, u32[]{:S(2)}) collective-permute-start(bf16[2,8,32]{2,1,0:T(8,128)(2,1)S(1)} %get-tuple-element.64), channel_id=1, source_target_pairs={{0,13},{1,12},{2,15},{3,14},{4,9},{5,8},{6,11},{7,10},{8,5},{9,4},... | collective-permute-start | bytes 3080 | tf_op jit(solution)/shard_map/ppermute | solution.py:23
  78.2 6.3 %collective-permute-start.13 = (bf16[2,8,32]{2,1,0:T(8,128)(2,1)S(1)}, bf16[2,8,32]{2,1,0:T(8,128)(2,1)S(1)}, u32[]{:S(2)}, u32[]{:S(2)}) collective-permute-start(bf16[2,8,32]{2,1,0:T(8,128)(2,1)S(1)} %get-tuple-element.63), channel_id=1, source_target_pairs={{0,14},{1,15},{2,12},{3,13},{4,10},{5,11},{6,8},{7,9},{8,6},{9,7},... | collective-permute-start | bytes 3080 | tf_op jit(solution)/shard_map/ppermute | solution.py:23
  78.7 5.8 %collective-permute-start.14 = (bf16[2,8,32]{2,1,0:T(8,128)(2,1)S(1)}, bf16[2,8,32]{2,1,0:T(8,128)(2,1)S(1)}, u32[]{:S(2)}, u32[]{:S(2)}) collective-permute-start(bf16[2,8,32]{2,1,0:T(8,128)(2,1)S(1)} %get-tuple-element.62), channel_id=1, source_target_pairs={{0,15},{1,14},{2,13},{3,12},{4,11},{5,10},{6,9},{7,8},{8,7},{9,6},... | collective-permute-start | bytes 3080 | tf_op jit(solution)/shard_map/ppermute | solution.py:23
  84.6 0.8 copy-start.5
  84.6 0.8 copy-start.6
